TPU v7x, 32 devices: a whole 2x2x4 slice. The times are simulated.
32 devices in a mesh: group: 4 (over y, x), dev: 8 (over z, core).
Axes of the slice: x: 2, y: 2, z: 4, core: 2. Of those that a mesh axis runs over, the one named last changes fastest.
Arguments:
- grid_state: bfloat16 [32768, 512], P(('group', 'dev')), may hold values from -6 to 6
- mesh_state: bfloat16 [4096, 512], P(('group', 'dev')), may hold values from -6 to 6
- encode_edge: bfloat16 [512, 512], replicated, may hold values from -0.25 to 0.25
- encode_first: bfloat16 [512, 512], replicated, may hold values from -0.25 to 0.25
- encode_second: bfloat16 [512, 512], replicated, may hold values from -0.25 to 0.25
- process_edge: bfloat16 [512, 512], replicated, may hold values from -0.25 to 0.25
- process_first: bfloat16 [512, 512], replicated, may hold values from -0.25 to 0.25
- process_second: bfloat16 [512, 512], replicated, may hold values from -0.25 to 0.25
- decode_edge: bfloat16 [512, 512], replicated, may hold values from -0.25 to 0.25
- decode_first: bfloat16 [512, 512], replicated, may hold values from -0.25 to 0.25
- decode_second: bfloat16 [512, 512], replicated, may hold values from -0.25 to 0.25
- encode_near: bfloat16 [3, 4096, 1024], P(None, ('group', 'dev')), may hold values from -0.09375 to 0.09375
- encode_live: int32 [3, 256], P(None, ('group', 'dev')), may hold values 0 or 1
- encode_far: bfloat16 [2, 4096, 1024], P(None, ('group', 'dev')), may hold values from -0.09375 to 0.09375
- encode_groups: int32 [2, 32], P(None, ('group', 'dev')), may hold values from 0 to 3, as said below
- process_near: bfloat16 [3, 4096, 128], P(None, ('group', 'dev')), may hold values from -0.25 to 0.25
- process_far: bfloat16 [2, 4096, 128], P(None, ('group', 'dev')), may hold values from -0.25 to 0.25
- process_groups: int32 [2, 32], P(None, ('group', 'dev')), may hold values from 0 to 3, as said below
- decode_near: bfloat16 [3, 32768, 128], P(None, ('group', 'dev')), may hold values from -0.3125 to 0.3125
- decode_live: int32 [3, 256], P(None, ('group', 'dev')), may hold values 0 or 1
Outputs:
- grid_next: bfloat16 [32768, 512], P(('group', 'dev'))
- mesh_next: bfloat16 [4096, 512], P(('group', 'dev'))
Inputs may be any that keep to these rules, and one draw needn't show every extreme that they name: `encode_groups`: for each device q the 2 entries of column q are distinct regions, none equal to q's own region q // 8. `process_groups`: for each device q the 2 entries of column q are distinct regions, none equal to q's own region q // 8.
All inputs are finite; a program needn't handle non-finite values. No bound on the sum of `encode_live` or of `decode_live` on one device may be relied on, other than what follows from the above.
Results may differ from a plain program's by a relative error of at most 0.013.
Values may be sent and summed in bfloat16 or wider, within the bound.
A program may use at most 64 MiB of HBM per device.

v0:
```python
import jax
import jax.numpy as jnp
from jax import lax
from jax.sharding import PartitionSpec as P


def shifted(value, axis, steps):
    count = lax.axis_size(axis)
    first, last = (max(0, -steps), min(count, count - steps))
    return lax.ppermute(value, axis, [(source, source + steps) for source in range(first, last)])


def padded_2(array, sides, width):
    for axis, dim in sides:
        size, length = (lax.axis_size(axis), array.shape[dim])
        up = [(i, (i + 1) % size) for i in range(size - 1)]
        down = [(j, i) for i, j in up]
        last = lax.slice_in_dim(array, length - width, length, axis=dim)
        first = lax.slice_in_dim(array, 0, width, axis=dim)
        before = lax.ppermute(last, axis, up)
        after = lax.ppermute(first, axis, down)
        array = jnp.concatenate([before, array, after], axis=dim)
    return array


def layer_norm(row_values):
    row_mean = jnp.mean(row_values, axis=-1, keepdims=True)
    centred = row_values - row_mean
    variance = jnp.mean(centred * centred, axis=-1, keepdims=True)
    return centred * lax.rsqrt(variance + 1e-05)


def node_update(residual_in, summed, weight_in, weight_out):
    normed = layer_norm(summed).astype(jnp.bfloat16)
    hidden = jax.nn.silu(jnp.dot(normed, weight_in, preferred_element_type=jnp.float32)).astype(
        jnp.bfloat16
    )
    updated = residual_in.astype(jnp.float32) + jnp.dot(
        hidden, weight_out, preferred_element_type=jnp.float32
    )
    return updated.astype(jnp.bfloat16)


def edge_messages(latents, weight):
    return jax.nn.silu(jnp.dot(latents, weight, preferred_element_type=jnp.float32)).astype(
        jnp.bfloat16
    )


def body(
    grid_state,
    mesh_state,
    encode_edge,
    encode_first,
    encode_second,
    process_edge,
    process_first,
    process_second,
    decode_edge,
    decode_first,
    decode_second,
    encode_near,
    encode_live,
    encode_far,
    encode_groups,
    process_near,
    process_far,
    process_groups,
    decode_near,
    decode_live,
):
    tile_rows = mesh_state.shape[0]
    tile_count = grid_state.shape[0] // tile_rows
    features = grid_state.shape[1]
    enc_msg = edge_messages(grid_state, encode_edge)
    stacked = enc_msg.reshape(tile_count, tile_rows, features)
    partials = []
    for offset in range(3):
        live_flag = encode_live[offset].astype(jnp.bfloat16)
        masked = (stacked * live_flag[:, None, None]).reshape(-1, features)
        partials.append(jnp.dot(encode_near[offset], masked, preferred_element_type=jnp.float32))
    from_below = shifted(partials[2].astype(jnp.bfloat16), "dev", 1)
    from_above = shifted(partials[0].astype(jnp.bfloat16), "dev", -1)
    own_part = lax.optimization_barrier(partials[1].astype(jnp.bfloat16)).astype(jnp.float32)
    near_sum = own_part + from_below.astype(jnp.float32) + from_above.astype(jnp.float32)
    far_parts = [
        jnp.dot(encode_far[index], enc_msg, preferred_element_type=jnp.float32)
        for index in range(encode_far.shape[0])
    ]
    block_count = tile_rows * lax.axis_size("group") // tile_rows
    slot_ids = jnp.arange(block_count, dtype=jnp.int32)
    partial_term = jnp.zeros((block_count, tile_rows, features), jnp.float32)
    for index in range(len(far_parts)):
        matches = (slot_ids == encode_groups[index, 0]).astype(jnp.float32)
        partial_term = partial_term + matches[:, None, None] * far_parts[index][None]
    far_sum = lax.psum_scatter(
        partial_term.reshape(tile_rows * lax.axis_size("group"), features).astype(jnp.bfloat16),
        "group",
        scatter_dimension=0,
        tiled=True,
    ).astype(jnp.float32)
    mesh_mid = node_update(mesh_state, near_sum + far_sum, encode_first, encode_second)
    proc_msg = edge_messages(mesh_mid, process_edge)
    padded = padded_2(proc_msg, (("dev", 0),), tile_rows)
    proc_sum = jnp.dot(process_near[0], padded[:tile_rows], preferred_element_type=jnp.float32)
    proc_sum = proc_sum + jnp.dot(process_near[1], proc_msg, preferred_element_type=jnp.float32)
    proc_sum = proc_sum + jnp.dot(
        process_near[2], padded[2 * tile_rows :], preferred_element_type=jnp.float32
    )
    running = proc_sum
    shard_rows = lax.all_gather(proc_msg, "group", axis=0, tiled=True)
    block_count = shard_rows.shape[0] // tile_rows
    for index in range(process_far.shape[0]):
        slot_index = process_groups[index, 0]
        is_inside = (slot_index >= 0) & (slot_index < block_count)
        picked = lax.dynamic_slice_in_dim(
            shard_rows, jnp.clip(slot_index, 0, block_count - 1) * tile_rows, tile_rows, 0
        )
        far_product = jnp.dot(process_far[index], picked, preferred_element_type=jnp.float32)
        running = running + jnp.where(is_inside, far_product, 0.0)
    proc_sum = running
    mesh_next = node_update(mesh_mid, proc_sum, process_first, process_second)
    dec_msg = edge_messages(mesh_next, decode_edge)
    dec_padded = padded_2(dec_msg, (("dev", 0),), tile_rows)
    sources = (dec_padded[:tile_rows], dec_msg, dec_padded[2 * tile_rows :])
    dec_sum = jnp.zeros((tile_count, tile_rows, features), jnp.float32)
    for offset in range(3):
        product = jnp.dot(decode_near[offset], sources[offset], preferred_element_type=jnp.float32)
        live_flag = decode_live[offset].astype(jnp.float32)
        dec_sum = (
            dec_sum + product.reshape(tile_count, tile_rows, features) * live_flag[:, None, None]
        )
    grid_next = node_update(grid_state, dec_sum.reshape(-1, features), decode_first, decode_second)
    return (grid_next, mesh_next)


def solution(mesh):
    return jax.shard_map(
        body,
        mesh=mesh,
        in_specs=(
            P(("group", "dev"), None),
            P(("group", "dev"), None),
            P(),
            P(),
            P(),
            P(),
            P(),
            P(),
            P(),
            P(),
            P(),
            P(None, ("group", "dev"), None),
            P(None, ("group", "dev")),
            P(None, ("group", "dev"), None),
            P(None, ("group", "dev")),
            P(None, ("group", "dev"), None),
            P(None, ("group", "dev"), None),
            P(None, ("group", "dev")),
            P(None, ("group", "dev"), None),
            P(None, ("group", "dev")),
        ),
        out_specs=(P(("group", "dev"), None), P(("group", "dev"), None)),
        check_vma=False,
    )
```

profile of v0, /device:TPU:1, one launch (start us, length us, event | category | flops | bytes accessed | tf_op | source)
XLA Modules:
  0.0 87.9 jit_solution(10558357425975127363)
XLA Ops:
  7.2 1.0 %copy-done = bf16[512,512]{1,0:T(8,128)(2,1)S(1)} copy-done((bf16[512,512]{1,0:T(8,128)(2,1)S(1)}, bf16[512,512]{1,0:T(8,128)(2,1)}, u32[]{:S(2)}) %copy-start) | copy-done | bytes 524312
  8.2 2.2 %multiply_convert_fusion.2 = bf16[1024,512]{1,0:T(8,128)(2,1)S(1)} fusion(bf16[1024,512]{1,0:T(8,128)(2,1)} %param.20, bf16[512,512]{1,0:T(8,128)(2,1)S(1)} %copy-done), kind=kOutput, calls=%fused_computation.5 | convolution fusion | flops 539492352 | bytes 2621440 | tf_op jit(solution)/shard_map/dot_general | solution.py:45
  10.5 0.5 convolution_bitcast_fusion.1
  10.9 0.5 convolution_bitcast_fusion
  11.4 0.6 fusion.73
  12.0 0.6 compare_convert_fusion
  12.7 0.7 compare_convert_fusion.1
  13.3 0.1 broadcast_bitcast_fusion.3
  13.4 0.2 mul.202
  13.6 0.2 mul.208
  13.8 0.3 fusion.10
  14.1 1.0 %copy.22 = bf16[512,512]{1,0:T(8,128)(2,1)} copy(bf16[512,512]{0,1:T(8,128)(2,1)S(1)} %fusion.10) | data formatting | bytes 1048576
  15.1 0.1 broadcast_bitcast_fusion.6
  15.2 0.7 fusion.6
  15.9 4.6 %collective-permute-start = (bf16[128,512]{0,1:T(8,128)(2,1)S(1)}, bf16[128,512]{0,1:T(8,128)(2,1)S(1)}, u32[]{:S(2)}, u32[]{:S(2)}) collective-permute-start(bf16[128,512]{0,1:T(8,128)(2,1)S(1)} %fusion.6), channel_id=1, source_target_pairs={{0,1},{1,2},{2,3},{3,4},{4,5},{5,6},{6,7},{8,9},{9,10},{10,11},{11... | collective-permute-start | bytes 393224 | tf_op jit(solution)/shard_map/ppermute | solution.py:10
  20.5 0.1 broadcast_bitcast_fusion.5
  20.6 0.7 fusion.7
  21.3 2.1 %collective-permute-start.1 = (bf16[128,512]{0,1:T(8,128)(2,1)S(1)}, bf16[128,512]{0,1:T(8,128)(2,1)S(1)}, u32[]{:S(2)}, u32[]{:S(2)}) collective-permute-start(bf16[128,512]{0,1:T(8,128)(2,1)S(1)} %fusion.7), channel_id=1, source_target_pairs={{1,0},{2,1},{3,2},{4,3},{5,4},{6,5},{7,6},{9,8},{10,9},{11,10},{12... | collective-permute-start | bytes 393224 | tf_op jit(solution)/shard_map/ppermute | solution.py:10
  23.3 0.6 fusion.72
  27.8 0.1 broadcast_bitcast_fusion.7
  27.9 0.7 fusion.5
  28.8 13.3 %reduce-scatter.4.cloned.1.call-done = bf16[128,512]{1,0:T(8,128)(2,1)} async-done(((bf16[512,512]{1,0:T(8,128)(2,1)}), bf16[128,512]{1,0:T(8,128)(2,1)}) %reduce-scatter.4.cloned.1.call-update) | async-done | bytes 131088
  42.0 1.0 %copy.23 = bf16[128,512]{0,1:T(8,128)(2,1)S(1)} copy(bf16[128,512]{1,0:T(8,128)(2,1)} %reduce-scatter.4.cloned.1.call-done) | data formatting | bytes 262144
  43.1 0.1 fusion.71
  43.2 0.1 multiply_reduce_fusion.2
  43.3 1.7 %fusion.3 = bf16[128,512]{1,0:T(8,128)(2,1)S(1)} fusion(bf16[512,512]{1,0:T(8,128)(2,1)} %param.24, bf16[128,512]{1,0:T(8,128)(2,1)S(1)} %copy-done.15, bf16[512,512]{1,0:T(8,128)(2,1)} %param.23, f32[128]{0:T(128)S(1)} %add_rsqrt_fusion.2, f32[128]{0:T(128)S(1)} %broadcast_multiply_fusion.2, bf16[128,512]{0,1:T(8,128)(2,1)S(1)} %copy.23, ...), kind=kOutput, calls=%fused_computation.16 | convolution fusion | flops 135397376 | bytes 1836032 | tf_op jit(solution)/shard_map/dot_general | solution.py:38
  45.1 0.3 multiply_convert_fusion.11
  45.4 8.1 %all_gather.3 = bf16[512,512]{1,0:T(8,128)(2,1)S(1)} all-gather(bf16[128,512]{1,0:T(8,128)(2,1)S(1)} %multiply_convert_fusion.11), channel_id=1, replica_groups=mesh['group'=4,'dev'=8] {'group'}, dimensions={0}, use_global_device_ids=true | all-gather | bytes 655360 | tf_op jit(solution)/shard_map/all_gather | solution.py:111
  53.5 5.3 %collective-permute-start.3 = (bf16[128,512]{1,0:T(8,128)(2,1)S(1)}, bf16[128,512]{1,0:T(8,128)(2,1)S(1)}, u32[]{:S(2)}, u32[]{:S(2)}) collective-permute-start(bf16[128,512]{1,0:T(8,128)(2,1)S(1)} %multiply_convert_fusion.11), channel_id=1, source_target_pairs={{1,0},{2,1},{3,2},{4,3},{5,4},{6,5},{7,6},{9,8},{10,9},{11,10},{12... | collective-permute-start | bytes 393224 | tf_op jit(solution)/shard_map/ppermute | solution.py:21
  58.8 3.0 %collective-permute-start.2 = (bf16[128,512]{1,0:T(8,128)(2,1)S(1)}, bf16[128,512]{1,0:T(8,128)(2,1)S(1)}, u32[]{:S(2)}, u32[]{:S(2)}) collective-permute-start(bf16[128,512]{1,0:T(8,128)(2,1)S(1)} %multiply_convert_fusion.11), channel_id=1, source_target_pairs={{0,1},{1,2},{2,3},{3,4},{4,5},{5,6},{6,7},{8,9},{9,10},{10,11},{11... | collective-permute-start | bytes 393224 | tf_op jit(solution)/shard_map/ppermute | solution.py:20
  61.8 0.2 fusion.58
  62.0 0.2 convolution_select_fusion.1
  62.3 0.2 convolution_select_fusion
  62.5 0.2 fusion.56
  62.7 1.0 %collective-permute-done.2 = bf16[128,512]{1,0:T(8,128)(2,1)S(1)} collective-permute-done((bf16[128,512]{1,0:T(8,128)(2,1)S(1)}, bf16[128,512]{1,0:T(8,128)(2,1)S(1)}, u32[]{:S(2)}, u32[]{:S(2)}) %collective-permute-start.2) | collective-permute-done | bytes 131104 | tf_op jit(solution)/shard_map/ppermute | solution.py:20
  63.7 0.3 fusion.74
  64.0 0.1 multiply_reduce_fusion.1
  64.1 0.5 fusion.4
  64.6 0.3 multiply_convert_fusion.9
  64.9 4.4 %collective-permute-start.4 = (bf16[128,512]{1,0:T(8,128)(2,1)S(1)}, bf16[128,512]{1,0:T(8,128)(2,1)S(1)}, u32[]{:S(2)}, u32[]{:S(2)}) collective-permute-start(bf16[128,512]{1,0:T(8,128)(2,1)S(1)} %multiply_convert_fusion.9), channel_id=1, source_target_pairs={{0,1},{1,2},{2,3},{3,4},{4,5},{5,6},{6,7},{8,9},{9,10},{10,11},{11... | collective-permute-start | bytes 393224 | tf_op jit(solution)/shard_map/ppermute | solution.py:20
  69.3 1.9 %collective-permute-start.5 = (bf16[128,512]{1,0:T(8,128)(2,1)S(1)}, bf16[128,512]{1,0:T(8,128)(2,1)S(1)}, u32[]{:S(2)}, u32[]{:S(2)}) collective-permute-start(bf16[128,512]{1,0:T(8,128)(2,1)S(1)} %multiply_convert_fusion.9), channel_id=1, source_target_pairs={{1,0},{2,1},{3,2},{4,3},{5,4},{6,5},{7,6},{9,8},{10,9},{11,10},{12... | collective-permute-start | bytes 393224 | tf_op jit(solution)/shard_map/ppermute | solution.py:21
  71.2 0.5 fusion.23
  71.7 0.5 fusion.25
  72.1 3.4 %collective-permute-done.5 = bf16[128,512]{1,0:T(8,128)(2,1)S(1)} collective-permute-done((bf16[128,512]{1,0:T(8,128)(2,1)S(1)}, bf16[128,512]{1,0:T(8,128)(2,1)S(1)}, u32[]{:S(2)}, u32[]{:S(2)}) %collective-permute-start.5) | collective-permute-done | bytes 131104 | tf_op jit(solution)/shard_map/ppermute | solution.py:21
  75.5 0.6 fusion.75
  76.2 0.3 multiply_reduce_fusion
  76.5 0.7 copy-done.14
  77.2 3.8 %add_convert_fusion = bf16[1024,512]{1,0:T(8,128)(2,1)} fusion(bf16[1024,512]{1,0:T(8,128)(2,1)} %param.20, bf16[512,512]{1,0:T(8,128)(2,1)S(1)} %copy-done.14, bf16[512,512]{1,0:T(8,128)(2,1)} %param.29, f32[512,1024]{1,0:T(8,128)S(1)} %get-tuple-element.15, f32[1024]{0:T(1024)S(1)} %add_rsqrt_fusion, f32[1024]{0:T(1024)S(1)} %broadcast_multiply_fusion), kind=kOutput, calls=%fused_computation.2 | convolution fusion | flops 1079508992 | bytes 5251072 | tf_op jit(solution)/shard_map/dot_general | solution.py:38
  (49 shorter events, 0.4 us)
Async XLA Ops:
  7.2 1.0 %copy-start = (bf16[512,512]{1,0:T(8,128)(2,1)S(1)}, bf16[512,512]{1,0:T(8,128)(2,1)}, u32[]{:S(2)}) copy-start(bf16[512,512]{1,0:T(8,128)(2,1)} %param.22) | copy-start | bytes 1572868
  7.2 3.3 %copy-start.2 = (bf16[2,128,1024]{2,1,0:T(8,128)(2,1)S(1)}, bf16[2,128,1024]{2,1,0:T(8,128)(2,1)}, u32[]{:S(2)}) copy-start(bf16[2,128,1024]{2,1,0:T(8,128)(2,1)} %param.33) | copy-start | bytes 1572868
  7.2 34.9 %reduce-scatter.4.cloned.1.call-start = ((), (), s32[]{:S(2)}) async-start(), calls=%async_computation.1 | async-start | bytes 655360
  10.4 1.0 %copy-start.6 = (s32[2,1]{0,1:T(1,128)S(1)}, s32[2,1]{0,1:T(1,128)}, u32[]{:S(2)}) copy-start(s32[2,1]{0,1:T(1,128)} %param.34) | copy-start | bytes 28
  13.8 1.3 %copy-start.5 = (s32[3,8]{1,0:T(4,128)S(1)}, s32[3,8]{1,0:T(4,128)}, u32[]{:S(2)}) copy-start(s32[3,8]{1,0:T(4,128)} %param.32) | copy-start | bytes 292
  13.8 1.4 %copy-start.9 = (bf16[3,128,1024]{2,1,0:T(8,128)(2,1)S(1)}, bf16[3,128,1024]{2,1,0:T(8,128)(2,1)}, u32[]{:S(2)}) copy-start(bf16[3,128,1024]{2,1,0:T(8,128)(2,1)} %param.31) | copy-start | bytes 2359300
  15.1 8.2 %copy-start.7 = (s32[2,1]{0,1:T(1,128)S(1)}, s32[2,1]{0,1:T(1,128)}, u32[]{:S(2)}) copy-start(s32[2,1]{0,1:T(1,128)} %param.37) | copy-start | bytes 28
  15.9 12.7 %copy-start.8 = (s32[3,8]{1,0:T(4,128)S(1)}, s32[3,8]{1,0:T(4,128)}, u32[]{:S(2)}) copy-start(s32[3,8]{1,0:T(4,128)} %param.39) | copy-start | bytes 292
  15.9 27.2 %collective-permute-start = (bf16[128,512]{0,1:T(8,128)(2,1)S(1)}, bf16[128,512]{0,1:T(8,128)(2,1)S(1)}, u32[]{:S(2)}, u32[]{:S(2)}) collective-permute-start(bf16[128,512]{0,1:T(8,128)(2,1)S(1)} %fusion.6), channel_id=1, source_target_pairs={{0,1},{1,2},{2,3},{3,4},{4,5},{5,6},{6,7},{8,9},{9,10},{10,11},{11... | collective-permute-start | bytes 393224 | tf_op jit(solution)/shard_map/ppermute | solution.py:10
  21.3 22.0 %copy-start.15 = (bf16[128,512]{1,0:T(8,128)(2,1)S(1)}, bf16[128,512]{1,0:T(8,128)(2,1)}, u32[]{:S(2)}) copy-start(bf16[128,512]{1,0:T(8,128)(2,1)} %param.21) | copy-start | bytes 393220
  21.3 21.8 %collective-permute-start.1 = (bf16[128,512]{0,1:T(8,128)(2,1)S(1)}, bf16[128,512]{0,1:T(8,128)(2,1)S(1)}, u32[]{:S(2)}, u32[]{:S(2)}) collective-permute-start(bf16[128,512]{0,1:T(8,128)(2,1)S(1)} %fusion.7), channel_id=1, source_target_pairs={{1,0},{2,1},{3,2},{4,3},{5,4},{6,5},{7,6},{9,8},{10,9},{11,10},{12... | collective-permute-start | bytes 393224 | tf_op jit(solution)/shard_map/ppermute | solution.py:10
  28.6 16.5 %copy-start.10 = (bf16[512,512]{1,0:T(8,128)(2,1)S(1)}, bf16[512,512]{1,0:T(8,128)(2,1)}, u32[]{:S(2)}) copy-start(bf16[512,512]{1,0:T(8,128)(2,1)} %param.25) | copy-start | bytes 1572868
  43.3 18.5 %copy-start.3 = (bf16[3,128,128]{2,1,0:T(8,128)(2,1)S(1)}, bf16[3,128,128]{2,1,0:T(8,128)(2,1)}, u32[]{:S(2)}) copy-start(bf16[3,128,128]{2,1,0:T(8,128)(2,1)} %param.35) | copy-start | bytes 294916
  43.3 18.7 %copy-start.4 = (bf16[2,128,128]{2,1,0:T(8,128)(2,1)S(1)}, bf16[2,128,128]{2,1,0:T(8,128)(2,1)}, u32[]{:S(2)}) copy-start(bf16[2,128,128]{2,1,0:T(8,128)(2,1)} %param.36) | copy-start | bytes 196612
  45.4 18.7 %copy-start.11 = (bf16[512,512]{1,0:T(8,128)(2,1)S(1)}, bf16[512,512]{1,0:T(8,128)(2,1)}, u32[]{:S(2)}) copy-start(bf16[512,512]{1,0:T(8,128)(2,1)} %param.27) | copy-start | bytes 1572868
  45.4 18.7 %copy-start.12 = (bf16[512,512]{1,0:T(8,128)(2,1)S(1)}, bf16[512,512]{1,0:T(8,128)(2,1)}, u32[]{:S(2)}) copy-start(bf16[512,512]{1,0:T(8,128)(2,1)} %param.26) | copy-start | bytes 1572868
  53.5 9.0 %collective-permute-start.3 = (bf16[128,512]{1,0:T(8,128)(2,1)S(1)}, bf16[128,512]{1,0:T(8,128)(2,1)S(1)}, u32[]{:S(2)}, u32[]{:S(2)}) collective-permute-start(bf16[128,512]{1,0:T(8,128)(2,1)S(1)} %multiply_convert_fusion.11), channel_id=1, source_target_pairs={{1,0},{2,1},{3,2},{4,3},{5,4},{6,5},{7,6},{9,8},{10,9},{11,10},{12... | collective-permute-start | bytes 393224 | tf_op jit(solution)/shard_map/ppermute | solution.py:21
  58.8 5.0 %collective-permute-start.2 = (bf16[128,512]{1,0:T(8,128)(2,1)S(1)}, bf16[128,512]{1,0:T(8,128)(2,1)S(1)}, u32[]{:S(2)}, u32[]{:S(2)}) collective-permute-start(bf16[128,512]{1,0:T(8,128)(2,1)S(1)} %multiply_convert_fusion.11), channel_id=1, source_target_pairs={{0,1},{1,2},{2,3},{3,4},{4,5},{5,6},{6,7},{8,9},{9,10},{10,11},{11... | collective-permute-start | bytes 393224 | tf_op jit(solution)/shard_map/ppermute | solution.py:20
  62.5 2.1 %copy-start.13 = (bf16[512,512]{1,0:T(8,128)(2,1)S(1)}, bf16[512,512]{1,0:T(8,128)(2,1)}, u32[]{:S(2)}) copy-start(bf16[512,512]{1,0:T(8,128)(2,1)} %param.28) | copy-start | bytes 1572868
  64.0 7.2 %copy-start.1 = (bf16[3,1024,128]{2,1,0:T(8,128)(2,1)S(1)}, bf16[3,1024,128]{2,1,0:T(8,128)(2,1)}, u32[]{:S(2)}) copy-start(bf16[3,1024,128]{2,1,0:T(8,128)(2,1)} %param.38) | copy-start | bytes 2359300
  64.6 7.5 %copy-start.16 = (bf16[128,512]{1,0:T(8,128)(2,1)}, bf16[128,512]{1,0:T(8,128)(2,1)S(1)}, u32[]{:S(2)}) copy-start(bf16[128,512]{1,0:T(8,128)(2,1)S(1)} %fusion.4) | copy-start | bytes 393220
  64.9 6.8 %collective-permute-start.4 = (bf16[128,512]{1,0:T(8,128)(2,1)S(1)}, bf16[128,512]{1,0:T(8,128)(2,1)S(1)}, u32[]{:S(2)}, u32[]{:S(2)}) collective-permute-start(bf16[128,512]{1,0:T(8,128)(2,1)S(1)} %multiply_convert_fusion.9), channel_id=1, source_target_pairs={{0,1},{1,2},{2,3},{3,4},{4,5},{5,6},{6,7},{8,9},{9,10},{10,11},{11... | collective-permute-start | bytes 393224 | tf_op jit(solution)/shard_map/ppermute | solution.py:20
  69.3 6.3 %collective-permute-start.5 = (bf16[128,512]{1,0:T(8,128)(2,1)S(1)}, bf16[128,512]{1,0:T(8,128)(2,1)S(1)}, u32[]{:S(2)}, u32[]{:S(2)}) collective-permute-start(bf16[128,512]{1,0:T(8,128)(2,1)S(1)} %multiply_convert_fusion.9), channel_id=1, source_target_pairs={{1,0},{2,1},{3,2},{4,3},{5,4},{6,5},{7,6},{9,8},{10,9},{11,10},{12... | collective-permute-start | bytes 393224 | tf_op jit(solution)/shard_map/ppermute | solution.py:21
  76.2 1.0 %copy-start.14 = (bf16[512,512]{1,0:T(8,128)(2,1)S(1)}, bf16[512,512]{1,0:T(8,128)(2,1)}, u32[]{:S(2)}) copy-start(bf16[512,512]{1,0:T(8,128)(2,1)} %param.30) | copy-start | bytes 1572868
Sparse Core Ops, SparseCore 0:
  15.2 26.7 reduce-scatter.3
where the time goes:
time: 88.4 us; the launch traced here: 87.9 us
  starting transfers between devices  21.2 us (24%)
  between operations  18.4 us (21%)
  waiting for transfers between devices  17.7 us (20%)
  matrix products  14.4 us (16%)
  blocking collectives  8.11 us (9%)
  local copies, waits for them, and re-layouts  5.82 us (7%)
  other arithmetic  2.18 us (2%)
    unnamed x2, waiting for transfers between devices  13.3 us
    all_gather x1, blocking collectives, body(): shard_rows = lax.all_gather(proc_msg, 'group', axis=0, tiled=True)  8.11 us
    ppermute x2, starting transfers between devices, padded_2(): before = lax.ppermute(last, axis, up)  7.38 us
    ppermute x2, starting transfers between devices, padded_2(): after = lax.ppermute(first, axis, down)  7.17 us
    ppermute x2, starting transfers between devices, shifted(): lax.ppermute(value, axis, [(source, source + steps) for source in range(f...  6.64 us
    dot_general x3, matrix products, node_update(): jnp.dot(hidden, weight_out, preferred_element_type=jnp.float32)  6 us
    unnamed x36, local copies, waits for them, and re-layouts  3.82 us
    ppermute x2, waiting for transfers between devices, padded_2(): after = lax.ppermute(first, axis, down)  3.42 us
  transfers between devices with their start and end apart: 7, of which 3 were waited for; matrix products, arithmetic and copies ran while one was open for 7% of the time, Pallas kernels for 0%

commit v1 on v0

v1 whole, which is shorter than its diff:
```python
import functools

import jax
import jax.numpy as jnp
from jax import lax
from jax.experimental import pallas as pl
from jax.experimental.pallas import tpu as pltpu
from jax.sharding import PartitionSpec as P

BF16 = jnp.bfloat16
F32 = jnp.float32
CHUNKS = 2


def silu(x):
    half = 0.5 * x
    return half + half * jnp.tanh(half)


def mm(a, b):
    return jnp.dot(a, b, preferred_element_type=F32)


def layer_norm(v):
    mean = jnp.mean(v, axis=-1, keepdims=True)
    cent = v - mean
    var = jnp.mean(cent * cent, axis=-1, keepdims=True)
    return cent * lax.rsqrt(var + 1e-05)


def partner(me, r, count):
    if count & (count - 1):
        return lax.rem(me + r, count), lax.rem(me + count - r, count)
    out, bit = me, 1
    while bit < count:
        if r & bit:
            out = out + bit * (1 - 2 * lax.rem(me // bit, 2))
        bit *= 2
    return out, out


def kernel(
    groups,
    devs,
    grid_h, mesh_h, ee_h, e1_h, e2_h, pe_h, p1_h, p2_h, de_h, d1_h, d2_h,
    en_h, el_h, ef_h, eg_h, pn_h, pf_h, pg_h, dn_h, dl_h,
    grid_o, mesh_o,
    gs, ms, wt, inc, el, eg, pn, pf, pg, dn, dl,
    em, fsend, frecv, nsend, nrecv, msend, mfrecv, mnrecv, dsend, dnrecv,
    own_near, proc_inc, dec_own, mesh_out, grid_out,
    load_sem, fs_sem, fr_sem, ns_sem, nr_sem, mfs_sem, mfr_sem, mns_sem, mnr_sem, ds_sem, dr_sem, out_sem,
):
    g = lax.axis_index("group")
    d = lax.axis_index("dev")
    rows, feats = ms.shape
    width = feats // CHUNKS
    far_count = groups - 1
    long_count = pf.shape[0]
    tiles = el.shape[1]
    peers = [partner(g, r, groups) for r in range(1, groups)]
    order = list(reversed(range(far_count)))
    not_first, not_last = d > 0, d < devs - 1
    sides = ((not_first, d - 1), (not_last, d + 1))

    def load(index, src, dst):
        return pltpu.make_async_copy(src, dst, load_sem.at[index])

    loads = [
        load(0, ee_h, wt.at[0]), load(1, grid_h, gs), load(2, eg_h, eg), load(3, ef_h, inc.at[pl.ds(0, long_count)]),
        load(4, el_h, el), load(5, en_h, inc.at[pl.ds(long_count, 3)]),
        load(6, mesh_h, ms), load(7, e1_h, wt.at[1]), load(8, e2_h, wt.at[2]), load(9, pe_h, wt.at[3]),
        load(10, pg_h, pg), load(11, pn_h, pn), load(12, pf_h, pf), load(13, p1_h, wt.at[4]), load(14, p2_h, wt.at[5]),
        load(15, de_h, wt.at[6]), load(16, dl_h, dl), load(17, dn_h, dn), load(18, d1_h, wt.at[7]), load(19, d2_h, wt.at[8]),
    ]
    for copy in loads[:6]:
        copy.start()

    barrier = pltpu.get_barrier_semaphore()
    for to, _ in peers:
        pl.semaphore_signal(barrier, inc=1, device_id=(to, d), device_id_type=pl.DeviceIdType.MESH)
    if groups & (groups - 1):
        for _, source in peers:
            pl.semaphore_signal(barrier, inc=1, device_id=(source, d), device_id_type=pl.DeviceIdType.MESH)
    for there, near in sides:
        @pl.when(there)
        def _():
            pl.semaphore_signal(barrier, inc=1, device_id=(g, near), device_id_type=pl.DeviceIdType.MESH)

    for copy in loads[6:]:
        copy.start()
    for side, (there, _) in enumerate(sides):
        @pl.when(jnp.logical_not(there))
        def _():
            for buf in (nrecv, mnrecv, dnrecv):
                for c in range(CHUNKS):
                    buf[c, side] = jnp.zeros((rows, width), BF16)

    def remote(src, dst, send, recv, to):
        return pltpu.make_async_remote_copy(
            src_ref=src, dst_ref=dst, send_sem=send, recv_sem=recv, device_id=to, device_id_type=pl.DeviceIdType.MESH
        )

    def far_copy(c, i):
        return remote(fsend.at[c, i], frecv.at[c, i], fs_sem.at[c, i], fr_sem.at[c, i], (peers[i][0], d))

    def near_copy(c, s):
        return remote(nsend.at[c, s], nrecv.at[c, 1 - s], ns_sem.at[c, s], nr_sem.at[c, 1 - s], (g, sides[s][1]))

    def near_in(c, s):
        return remote(nsend.at[c, s], nrecv.at[c, s], ns_sem.at[c, s], nr_sem.at[c, s], (g, sides[s][1]))

    def mfar_copy(c, i):
        return remote(msend.at[c], mfrecv.at[c, i], mfs_sem.at[c, i], mfr_sem.at[c, i], (peers[i][0], d))

    def mnear_copy(c, s):
        return remote(msend.at[c], mnrecv.at[c, 1 - s], mns_sem.at[c, s], mnr_sem.at[c, 1 - s], (g, sides[s][1]))

    def mnear_in(c, s):
        return remote(msend.at[c], mnrecv.at[c, s], mns_sem.at[c, s], mnr_sem.at[c, s], (g, sides[s][1]))

    def dec_copy(c, s):
        return remote(dsend.at[c], dnrecv.at[c, 1 - s], ds_sem.at[c, s], dr_sem.at[c, 1 - s], (g, sides[s][1]))

    def dec_in(c, s):
        return remote(dsend.at[c], dnrecv.at[c, s], ds_sem.at[c, s], dr_sem.at[c, s], (g, sides[s][1]))

    def start_side(copy, c):
        for s, (there, _) in enumerate(sides):
            @pl.when(there)
            def _():
                copy(c, s).start()

    def wait_side(copy, c, s):
        @pl.when(sides[s][0])
        def _():
            copy(c, s).wait_recv()

    loads[0].wait()
    loads[1].wait()
    step = 2 * rows
    for c in range(CHUNKS):
        cols = pl.ds(c * width, width)

        def edge(i, carry):
            at = pl.ds(pl.multiple_of(i * step, step), step)
            em[c, at, :] = silu(mm(gs[at, :], wt[0, :, cols])).astype(BF16)
            return carry

        lax.fori_loop(0, gs.shape[0] // step, edge, 0)
        if c == 0:
            for copy in loads[2:4]:
                copy.wait()
        far = [mm(inc[i], em[c]) for i in range(long_count)]
        if c == 0:
            pl.semaphore_wait(
                barrier,
                far_count * (1 if groups & (groups - 1) == 0 else 2) + jnp.where(not_first, 1, 0) + jnp.where(not_last, 1, 0),
            )
        for i in order:
            total = None
            for index in range(long_count):
                flag = jnp.where(eg[index, 0] == peers[i][0], 1.0, 0.0).astype(F32)
                term = far[index] * flag
                total = term if total is None else total + term
            fsend[c, i] = total.astype(BF16)
            far_copy(c, i).start()
        if c == 0:
            for copy in loads[4:6]:
                copy.wait()
            for k in range(3):
                for t in range(tiles):
                    flag = el[k, t].astype(F32).astype(BF16)
                    at = pl.ds(t * rows, rows)
                    inc[long_count + k, :, at] = inc[long_count + k, :, at] * flag
        for s, k in ((0, 0), (1, 2)):
            nsend[c, s] = mm(inc[long_count + k], em[c]).astype(BF16)
        start_side(near_copy, c)
        own_near[:, cols] = mm(inc[long_count + 1], em[c]).astype(BF16)

    for copy in loads[6:18]:
        copy.wait()
    for i in range(far_count):
        total = None
        for index in range(long_count):
            flag = jnp.where(pg[index, 0] == peers[i][1], 1.0, 0.0).astype(F32)
            term = pf[index].astype(F32) * flag
            total = term if total is None else total + term
        proc_inc[i] = total.astype(BF16)
    for k in range(3):
        for t in range(tiles):
            at = pl.ds(t * rows, rows)
            dn[k, at, :] = dn[k, at, :] * dl[k, t].astype(F32).astype(BF16)

    for copy in loads[18:]:
        copy.wait()

    def node_update(residual, summed, first, second):
        hidden = silu(mm(layer_norm(summed).astype(BF16), wt[first])).astype(BF16)
        return (residual.astype(F32) + mm(hidden, wt[second])).astype(BF16)

    parts = []
    for c in range(CHUNKS):
        total = own_near[:, pl.ds(c * width, width)].astype(F32)
        for s in range(2):
            wait_side(near_in, c, s)
            total = total + nrecv[c, s].astype(F32)
        for i in order:
            far_copy(c, i).wait_recv()
            total = total + frecv[c, i].astype(F32)
        parts.append(total)
    mesh_mid = node_update(ms[...], jnp.concatenate(parts, axis=1), 1, 2)

    for c in range(CHUNKS):
        msend[c] = silu(mm(mesh_mid, wt[3, :, pl.ds(c * width, width)])).astype(BF16)
        for i in order:
            mfar_copy(c, i).start()
        start_side(mnear_copy, c)
    parts = []
    for c in range(CHUNKS):
        total = mm(pn[1], msend[c])
        for s in range(2):
            wait_side(mnear_in, c, s)
            total = total + mm(pn[2 * s], mnrecv[c, s])
        for i in order:
            mfar_copy(c, i).wait_recv()
            total = total + mm(proc_inc[i], mfrecv[c, i])
        parts.append(total)
    mesh_next = node_update(mesh_mid, jnp.concatenate(parts, axis=1), 4, 5)
    mesh_out[...] = mesh_next

    for c in range(CHUNKS):
        dsend[c] = silu(mm(mesh_next, wt[6, :, pl.ds(c * width, width)])).astype(BF16)
        start_side(dec_copy, c)
    mesh_copy = pltpu.make_async_copy(mesh_out, mesh_o, out_sem.at[0])
    mesh_copy.start()

    def own_part(i, carry):
        at = pl.ds(pl.multiple_of(i * step, step), step)
        for c in range(CHUNKS):
            dec_own[at, pl.ds(c * width, width)] = mm(dn[1, at, :], dsend[c])
        return carry

    count = gs.shape[0] // step
    lax.fori_loop(0, count, own_part, 0)
    for c in range(CHUNKS):
        for s in range(2):
            wait_side(dec_in, c, s)
    outs = []
    for i in range(count):
        at = pl.ds(i * step, step)
        sums = []
        for c in range(CHUNKS):
            total = dec_own[at, pl.ds(c * width, width)]
            for s in range(2):
                total = total + mm(dn[2 * s, at, :], dnrecv[c, s])
            sums.append(total)
        grid_out[at, :] = node_update(gs[at, :], jnp.concatenate(sums, axis=1), 7, 8)
        copy = pltpu.make_async_copy(grid_out.at[at], grid_o.at[at], out_sem.at[1 + i])
        copy.start()
        outs.append(copy)

    for c in range(CHUNKS):
        for i in range(far_count):
            far_copy(c, i).wait_send()
            mfar_copy(c, i).wait_send()
        for s, (there, _) in enumerate(sides):
            @pl.when(there)
            def _():
                near_copy(c, s).wait_send()
                mnear_copy(c, s).wait_send()
                dec_copy(c, s).wait_send()
    mesh_copy.wait()
    for copy in outs:
        copy.wait()


def body(groups, devs, *args):
    grid_state, mesh_state = args[0], args[1]
    encode_live, encode_far, encode_groups = args[12], args[13], args[14]
    process_far, process_groups, decode_near, decode_live = args[16], args[17], args[18], args[19]
    grid_rows, feats = grid_state.shape
    rows = mesh_state.shape[0]
    width = feats // CHUNKS
    far_count = groups - 1
    long_count = encode_far.shape[0]

    def vmem(*shape, dtype=BF16):
        return pltpu.VMEM(shape, dtype)

    dma = pltpu.SemaphoreType.DMA
    block = (rows, width)
    scratch = [
        vmem(grid_rows, feats), vmem(rows, feats), vmem(9, feats, feats), vmem(3 + long_count, rows, grid_rows),
        pltpu.SMEM(encode_live.shape, jnp.int32), pltpu.SMEM(encode_groups.shape, jnp.int32),
        vmem(3, rows, rows), vmem(*process_far.shape), pltpu.SMEM(process_groups.shape, jnp.int32),
        vmem(*decode_near.shape), pltpu.SMEM(decode_live.shape, jnp.int32),
        vmem(CHUNKS, grid_rows, width),
        vmem(CHUNKS, far_count, *block), vmem(CHUNKS, far_count, *block), vmem(CHUNKS, 2, *block), vmem(CHUNKS, 2, *block),
        vmem(CHUNKS, *block), vmem(CHUNKS, far_count, *block), vmem(CHUNKS, 2, *block),
        vmem(CHUNKS, *block), vmem(CHUNKS, 2, *block),
        vmem(rows, feats), vmem(far_count, rows, rows), vmem(grid_rows, feats, dtype=F32), vmem(rows, feats),
        vmem(grid_rows, feats),
        dma((20,)), dma((CHUNKS, far_count)), dma((CHUNKS, far_count)), dma((CHUNKS, 2)), dma((CHUNKS, 2)),
        dma((CHUNKS, far_count)), dma((CHUNKS, far_count)), dma((CHUNKS, 2)), dma((CHUNKS, 2)),
        dma((CHUNKS, 2)), dma((CHUNKS, 2)), dma((1 + grid_rows // (2 * rows),)),
    ]
    hbm = pl.BlockSpec(memory_space=pl.ANY)
    return pl.pallas_call(
        functools.partial(kernel, groups, devs),
        out_shape=(
            jax.ShapeDtypeStruct(grid_state.shape, BF16),
            jax.ShapeDtypeStruct(mesh_state.shape, BF16),
        ),
        in_specs=[hbm] * len(args),
        out_specs=(hbm, hbm),
        scratch_shapes=scratch,
        compiler_params=pltpu.CompilerParams(collective_id=0, has_side_effects=True),
        name="step",
    )(*args)


def solution(mesh):
    both = ("group", "dev")
    row, whole, second = P(both, None), P(), P(None, both, None)
    flags = P(None, both)
    return jax.shard_map(
        functools.partial(body, mesh.shape["group"], mesh.shape["dev"]),
        mesh=mesh,
        in_specs=(
            row, row, whole, whole, whole, whole, whole, whole, whole, whole, whole,
            second, flags, second, flags, second, second, flags, second, flags,
        ),
        out_specs=(row, row),
        check_vma=False,
    )
```

time: 88.4 us -> 35.8 us (0.40)
  Pallas kernels: 0 us -> 30.1 us
  starting transfers between devices: 21.2 us -> 0 us
  between operations: 18.4 us -> 0.66 us
  waiting for transfers between devices: 17.7 us -> 0 us
  matrix products: 14.4 us -> 0 us
  blocking collectives: 8.11 us -> 0 us
  other arithmetic: 2.18 us -> 0 us
  local copies, waits for them, and re-layouts: 5.82 us -> 4.91 us
    pallas_call x0 -> x1, Pallas kernels: none -> 30.1 us  [body(): pl.pallas_call(functools.partial(kernel, groups, devs), out_shape=(jax.Sh...]
    ppermute x6 -> x0, starting transfers between devices: 21.2 us -> none  [the longest x2 7.38 us: padded_2(): before = lax.ppermute(last, axis, up)]
    dot_general x19 -> x0, matrix products: 14.4 us -> none  [the longest x3 6 us: node_update(): jnp.dot(hidden, weight_out, preferred_element_type=jnp.float32)]
    unnamed x2 -> x0, waiting for transfers between devices: 13.3 us -> none
    all_gather x1 -> x0, blocking collectives: 8.11 us -> none  [body(): shard_rows = lax.all_gather(proc_msg, 'group', axis=0, tiled=True)]
    ppermute x6 -> x0, waiting for transfers between devices: 4.44 us -> none  [the longest x2 3.42 us: padded_2(): after = lax.ppermute(first, axis, down)]
    convert_element_type x4 -> x0, other arithmetic: 1.57 us -> none  [the longest x2 1.3 us: body(): matches = (slot_ids == encode_groups[index, 0]).astype(jnp.float32)]
    slice x2 -> x0, local copies, waits for them, and re-layouts: 1.2 us -> none  [the longest x1 0.62 us: body(): slot_index = process_groups[index, 0]]
  transfers between devices with their start and end apart: 7 -> 0, of which waited for: 3 -> 0; matrix products, arithmetic and copies ran while one was open for 7% -> 0% of each run, Pallas kernels for 0% -> 0%
where the time goes in v1:
time: 35.8 us; the launch traced here: 35.7 us
  Pallas kernels  30.1 us (84%)
  local copies, waits for them, and re-layouts  4.91 us (14%)
  between operations  0.66 us (2%)
    pallas_call x1, Pallas kernels, body(): pl.pallas_call(functools.partial(kernel, groups, devs), out_shape=(jax.Sh...  30.1 us
    unnamed x8, local copies, waits for them, and re-layouts  4.91 us

profile of v1, /device:TPU:1, one launch (start us, length us, event | category | flops | bytes accessed | tf_op | source)
XLA Modules:
  0.0 35.7 jit_solution(11061998593575625113)
XLA Ops:
  0.6 0.0 copy-start.1
  0.6 1.3 %copy.22.eg_h = s32[2,1]{1,0:T(2,128)} copy(s32[2,1]{0,1:T(1,128)} %param.34) | data formatting | bytes 16 | tf_op args[14]
  1.9 0.0 copy-done.1
  1.9 0.6 %copy.23.pg_h = s32[2,1]{1,0:T(2,128)} copy(s32[2,1]{0,1:T(1,128)S(1)} %copy-done.1) | data formatting | bytes 16 | tf_op args[17]
  2.6 30.1 %step.1 = (bf16[1024,512]{1,0:T(8,128)(2,1)}, bf16[128,512]{1,0:T(8,128)(2,1)}) custom-call(bf16[1024,512]{1,0:T(8,128)(2,1)} %grid_h.1, bf16[128,512]{1,0:T(8,128)(2,1)} %mesh_h.1, bf16[512,512]{1,0:T(8,128)(2,1)} %ee_h.1, bf16[512,512]{1,0:T(8,128)(2,1)} %e1_h.1, bf16[512,512]{1,0:T(8,128)(2,1)} %e2_h.1, bf16[512,512]{1,0:T(8,128)(2,1)} %pe_h.1, ...), custom_call_target="tpu_custom_call" | custom-call | tf_op jit(solution)/shard_map/step/pallas_call | solution.py:308
  32.7 0.0 copy-start
  32.7 2.3 %copy.26 = bf16[1024,512]{1,0:T(8,128)(2,1)} copy(bf16[1024,512]{1,0:T(8,128)(2,1)} %get-tuple-element.4) | data formatting | bytes 2097152
  35.0 0.0 copy-done
  35.0 0.7 %copy.27 = bf16[128,512]{1,0:T(8,128)(2,1)} copy(bf16[128,512]{1,0:T(8,128)(2,1)S(1)} %copy-done) | data formatting | bytes 262144
Async XLA Ops:
  0.6 1.3 %copy-start.1 = (s32[2,1]{0,1:T(1,128)S(1)}, s32[2,1]{0,1:T(1,128)}, u32[]{:S(2)}) copy-start(s32[2,1]{0,1:T(1,128)} %param.37) | copy-start | bytes 28
  32.7 2.3 %copy-start = (bf16[128,512]{1,0:T(8,128)(2,1)S(1)}, bf16[128,512]{1,0:T(8,128)(2,1)}, u32[]{:S(2)}) copy-start(bf16[128,512]{1,0:T(8,128)(2,1)} %get-tuple-element.5) | copy-start | bytes 393220

commit v2 on v1

--- a/solution.py
+++ b/solution.py
@@ -46,9 +46,9 @@
     en_h, el_h, ef_h, eg_h, pn_h, pf_h, pg_h, dn_h, dl_h,
     grid_o, mesh_o,
     gs, ms, wt, inc, el, eg, pn, pf, pg, dn, dl,
-    em, fsend, frecv, nsend, nrecv, msend, mfrecv, mnrecv, dsend, dnrecv,
+    em, fheld, fsend, frecv, nsend, nrecv, msend, mfrecv, mnrecv, dsend, dnrecv,
     own_near, proc_inc, dec_own, mesh_out, grid_out,
-    load_sem, fs_sem, fr_sem, ns_sem, nr_sem, mfs_sem, mfr_sem, mns_sem, mnr_sem, ds_sem, dr_sem, out_sem,
+    load_sem, grid_sem, fs_sem, fr_sem, ns_sem, nr_sem, mfs_sem, mfr_sem, mns_sem, mnr_sem, ds_sem, dr_sem, out_sem,
 ):
     g = lax.axis_index("group")
     d = lax.axis_index("dev")
@@ -59,6 +59,15 @@
     tiles = el.shape[1]
     peers = [partner(g, r, groups) for r in range(1, groups)]
     order = list(reversed(range(far_count)))
+    relay = groups == 4
+    halves = fsend.shape[1]
+    piece_rows = rows // halves
+    if relay:
+        greeted = [to for to, _ in peers[:2]]
+    elif groups & (groups - 1):
+        greeted = [to for to, _ in peers] + [source for _, source in peers]
+    else:
+        greeted = [to for to, _ in peers]
     not_first, not_last = d > 0, d < devs - 1
     sides = ((not_first, d - 1), (not_last, d + 1))
 
@@ -66,28 +75,32 @@
         return pltpu.make_async_copy(src, dst, load_sem.at[index])
 
     loads = [
-        load(0, ee_h, wt.at[0]), load(1, grid_h, gs), load(2, eg_h, eg), load(3, ef_h, inc.at[pl.ds(0, long_count)]),
+        load(0, ee_h, wt.at[0]), load(2, eg_h, eg), load(3, ef_h, inc.at[pl.ds(0, long_count)]),
         load(4, el_h, el), load(5, en_h, inc.at[pl.ds(long_count, 3)]),
         load(6, mesh_h, ms), load(7, e1_h, wt.at[1]), load(8, e2_h, wt.at[2]), load(9, pe_h, wt.at[3]),
         load(10, pg_h, pg), load(11, pn_h, pn), load(12, pf_h, pf), load(13, p1_h, wt.at[4]), load(14, p2_h, wt.at[5]),
         load(15, de_h, wt.at[6]), load(16, dl_h, dl), load(17, dn_h, dn), load(18, d1_h, wt.at[7]), load(19, d2_h, wt.at[8]),
     ]
-    for copy in loads[:6]:
+    step = 2 * rows
+    count = gs.shape[0] // step
+    grid_loads = [
+        pltpu.make_async_copy(grid_h.at[pl.ds(i * step, step)], gs.at[pl.ds(i * step, step)], grid_sem.at[i])
+        for i in range(count)
+    ]
+    loads[0].start()
+    for copy in grid_loads:
         copy.start()
+    for copy in loads[1:3]:
+        copy.start()
 
     barrier = pltpu.get_barrier_semaphore()
-    for to, _ in peers:
+    for to in greeted:
         pl.semaphore_signal(barrier, inc=1, device_id=(to, d), device_id_type=pl.DeviceIdType.MESH)
-    if groups & (groups - 1):
-        for _, source in peers:
-            pl.semaphore_signal(barrier, inc=1, device_id=(source, d), device_id_type=pl.DeviceIdType.MESH)
     for there, near in sides:
         @pl.when(there)
         def _():
             pl.semaphore_signal(barrier, inc=1, device_id=(g, near), device_id_type=pl.DeviceIdType.MESH)
 
-    for copy in loads[6:]:
-        copy.start()
     for side, (there, _) in enumerate(sides):
         @pl.when(jnp.logical_not(there))
         def _():
@@ -100,8 +113,15 @@
             src_ref=src, dst_ref=dst, send_sem=send, recv_sem=recv, device_id=to, device_id_type=pl.DeviceIdType.MESH
         )
 
-    def far_copy(c, i):
-        return remote(fsend.at[c, i], frecv.at[c, i], fs_sem.at[c, i], fr_sem.at[c, i], (peers[i][0], d))
+    def first_axis(h):
+        return h % 2
+
+    def far_copy(c, h, i):
+        to = i
+        if relay:
+            to = first_axis(h) if i < 2 else 1 - first_axis(h)
+        at = (c, h, i)
+        return remote(fsend.at[at], frecv.at[at], fs_sem.at[at], fr_sem.at[at], (peers[to][0], d))
 
     def near_copy(c, s):
         return remote(nsend.at[c, s], nrecv.at[c, 1 - s], ns_sem.at[c, s], nr_sem.at[c, 1 - s], (g, sides[s][1]))
@@ -109,8 +129,12 @@
     def near_in(c, s):
         return remote(nsend.at[c, s], nrecv.at[c, s], ns_sem.at[c, s], nr_sem.at[c, s], (g, sides[s][1]))
 
-    def mfar_copy(c, i):
-        return remote(msend.at[c], mfrecv.at[c, i], mfs_sem.at[c, i], mfr_sem.at[c, i], (peers[i][0], d))
+    def mfar_copy(c, h, i):
+        at = pl.ds(h * piece_rows, piece_rows)
+        source, to = msend.at[c, at], i
+        if relay and i == 2:
+            source, to = mfrecv.at[c, first_axis(h), at], 1 - first_axis(h)
+        return remote(source, mfrecv.at[c, i, at], mfs_sem.at[c, h, i], mfr_sem.at[c, h, i], (peers[to][0], d))
 
     def mnear_copy(c, s):
         return remote(msend.at[c], mnrecv.at[c, 1 - s], mns_sem.at[c, s], mnr_sem.at[c, 1 - s], (g, sides[s][1]))
@@ -136,36 +160,46 @@
             copy(c, s).wait_recv()
 
     loads[0].wait()
-    loads[1].wait()
-    step = 2 * rows
     for c in range(CHUNKS):
         cols = pl.ds(c * width, width)
-
-        def edge(i, carry):
-            at = pl.ds(pl.multiple_of(i * step, step), step)
+        for i in range(count):
+            if c == 0:
+                grid_loads[i].wait()
+            at = pl.ds(i * step, step)
             em[c, at, :] = silu(mm(gs[at, :], wt[0, :, cols])).astype(BF16)
-            return carry
-
-        lax.fori_loop(0, gs.shape[0] // step, edge, 0)
         if c == 0:
-            for copy in loads[2:4]:
+            for copy in loads[3:]:
+                copy.start()
+            for copy in loads[1:3]:
                 copy.wait()
         far = [mm(inc[i], em[c]) for i in range(long_count)]
-        if c == 0:
-            pl.semaphore_wait(
-                barrier,
-                far_count * (1 if groups & (groups - 1) == 0 else 2) + jnp.where(not_first, 1, 0) + jnp.where(not_last, 1, 0),
-            )
-        for i in order:
+
+        def toward(i):
             total = None
             for index in range(long_count):
-                flag = jnp.where(eg[index, 0] == peers[i][0], 1.0, 0.0).astype(F32)
+                flag = jnp.where(eg[0, index] == peers[i][0], 1.0, 0.0).astype(F32)
                 term = far[index] * flag
                 total = term if total is None else total + term
-            fsend[c, i] = total.astype(BF16)
-            far_copy(c, i).start()
+            return total
+
         if c == 0:
-            for copy in loads[4:6]:
+            pl.semaphore_wait(barrier, len(greeted) + jnp.where(not_first, 1, 0) + jnp.where(not_last, 1, 0))
+        if relay:
+            totals = [toward(i) for i in range(far_count)]
+            for kind in range(2):
+                for h in range(halves):
+                    at = slice(h * piece_rows, (h + 1) * piece_rows)
+                    axis = first_axis(h)
+                    fsend[c, h, kind] = totals[2 if kind == 0 else axis][at].astype(BF16)
+                    far_copy(c, h, kind).start()
+                    if kind == 0:
+                        fheld[c, h] = totals[1 - axis][at]
+        else:
+            for i in order:
+                fsend[c, 0, i] = toward(i).astype(BF16)
+                far_copy(c, 0, i).start()
+        if c == 0:
+            for copy in loads[3:5]:
                 copy.wait()
             for k in range(3):
                 for t in range(tiles):
@@ -177,12 +211,19 @@
         start_side(near_copy, c)
         own_near[:, cols] = mm(inc[long_count + 1], em[c]).astype(BF16)
 
-    for copy in loads[6:18]:
+    if relay:
+        for c in range(CHUNKS):
+            for h in range(halves):
+                far_copy(c, h, 0).wait_recv()
+                fsend[c, h, 2] = (fheld[c, h] + frecv[c, h, 0].astype(F32)).astype(BF16)
+                far_copy(c, h, 2).start()
+
+    for copy in loads[5:17]:
         copy.wait()
     for i in range(far_count):
         total = None
         for index in range(long_count):
-            flag = jnp.where(pg[index, 0] == peers[i][1], 1.0, 0.0).astype(F32)
+            flag = jnp.where(pg[0, index] == peers[i][1], 1.0, 0.0).astype(F32)
             term = pf[index].astype(F32) * flag
             total = term if total is None else total + term
         proc_inc[i] = total.astype(BF16)
@@ -191,7 +232,7 @@
             at = pl.ds(t * rows, rows)
             dn[k, at, :] = dn[k, at, :] * dl[k, t].astype(F32).astype(BF16)
 
-    for copy in loads[18:]:
+    for copy in loads[17:]:
         copy.wait()
 
     def node_update(residual, summed, first, second):
@@ -204,27 +245,45 @@
         for s in range(2):
             wait_side(near_in, c, s)
             total = total + nrecv[c, s].astype(F32)
-        for i in order:
-            far_copy(c, i).wait_recv()
-            total = total + frecv[c, i].astype(F32)
-        parts.append(total)
+        pieces = []
+        for h in range(halves):
+            piece = total[h * piece_rows:(h + 1) * piece_rows]
+            for i in (1, 2) if relay else order:
+                far_copy(c, h, i).wait_recv()
+                piece = piece + frecv[c, h, i].astype(F32)
+            pieces.append(piece)
+        parts.append(jnp.concatenate(pieces, axis=0))
     mesh_mid = node_update(ms[...], jnp.concatenate(parts, axis=1), 1, 2)
 
     for c in range(CHUNKS):
         msend[c] = silu(mm(mesh_mid, wt[3, :, pl.ds(c * width, width)])).astype(BF16)
-        for i in order:
-            mfar_copy(c, i).start()
+        if not relay:
+            for i in order:
+                mfar_copy(c, 0, i).start()
+        else:
+            for h in range(halves):
+                mfar_copy(c, h, first_axis(h)).start()
         start_side(mnear_copy, c)
-    parts = []
-    for c in range(CHUNKS):
-        total = mm(pn[1], msend[c])
+    if relay:
+        for c in range(CHUNKS):
+            for h in range(halves):
+                mfar_copy(c, h, 1 - first_axis(h)).start()
+    parts = [mm(pn[1], msend[c]) for c in range(CHUNKS)]
+    if relay:
+        for c in range(CHUNKS):
+            for h in range(halves):
+                mfar_copy(c, h, first_axis(h)).wait_recv()
+                mfar_copy(c, h, 2).start()
+    for c in range(CHUNKS):
         for s in range(2):
             wait_side(mnear_in, c, s)
-            total = total + mm(pn[2 * s], mnrecv[c, s])
-        for i in order:
-            mfar_copy(c, i).wait_recv()
-            total = total + mm(proc_inc[i], mfrecv[c, i])
-        parts.append(total)
+            parts[c] = parts[c] + mm(pn[2 * s], mnrecv[c, s])
+    for i in range(far_count) if relay else order:
+        for c in range(CHUNKS):
+            for h in range(halves):
+                if not relay or i != first_axis(h):
+                    mfar_copy(c, h, i).wait_recv()
+            parts[c] = parts[c] + mm(proc_inc[i], mfrecv[c, i])
     mesh_next = node_update(mesh_mid, jnp.concatenate(parts, axis=1), 4, 5)
     mesh_out[...] = mesh_next
 
@@ -240,7 +299,6 @@
             dec_own[at, pl.ds(c * width, width)] = mm(dn[1, at, :], dsend[c])
         return carry
 
-    count = gs.shape[0] // step
     lax.fori_loop(0, count, own_part, 0)
     for c in range(CHUNKS):
         for s in range(2):
@@ -261,8 +319,9 @@
 
     for c in range(CHUNKS):
         for i in range(far_count):
-            far_copy(c, i).wait_send()
-            mfar_copy(c, i).wait_send()
+            for h in range(halves):
+                far_copy(c, h, i).wait_send()
+                mfar_copy(c, h, i).wait_send()
         for s, (there, _) in enumerate(sides):
             @pl.when(there)
             def _():
@@ -276,6 +335,8 @@
 
 def body(groups, devs, *args):
     grid_state, mesh_state = args[0], args[1]
+    args = list(args)
+    args[14], args[17] = args[14].T, args[17].T
     encode_live, encode_far, encode_groups = args[12], args[13], args[14]
     process_far, process_groups, decode_near, decode_live = args[16], args[17], args[18], args[19]
     grid_rows, feats = grid_state.shape
@@ -288,6 +349,9 @@
         return pltpu.VMEM(shape, dtype)
 
     dma = pltpu.SemaphoreType.DMA
+    halves = 2 if groups == 4 else 1
+    pieces = (CHUNKS, halves, far_count)
+    piece = (rows // halves, width)
     block = (rows, width)
     scratch = [
         vmem(grid_rows, feats), vmem(rows, feats), vmem(9, feats, feats), vmem(3 + long_count, rows, grid_rows),
@@ -295,13 +359,14 @@
         vmem(3, rows, rows), vmem(*process_far.shape), pltpu.SMEM(process_groups.shape, jnp.int32),
         vmem(*decode_near.shape), pltpu.SMEM(decode_live.shape, jnp.int32),
         vmem(CHUNKS, grid_rows, width),
-        vmem(CHUNKS, far_count, *block), vmem(CHUNKS, far_count, *block), vmem(CHUNKS, 2, *block), vmem(CHUNKS, 2, *block),
+        vmem(CHUNKS, halves, *piece, dtype=F32), vmem(*pieces, *piece), vmem(*pieces, *piece),
+        vmem(CHUNKS, 2, *block), vmem(CHUNKS, 2, *block),
         vmem(CHUNKS, *block), vmem(CHUNKS, far_count, *block), vmem(CHUNKS, 2, *block),
         vmem(CHUNKS, *block), vmem(CHUNKS, 2, *block),
         vmem(rows, feats), vmem(far_count, rows, rows), vmem(grid_rows, feats, dtype=F32), vmem(rows, feats),
         vmem(grid_rows, feats),
-        dma((20,)), dma((CHUNKS, far_count)), dma((CHUNKS, far_count)), dma((CHUNKS, 2)), dma((CHUNKS, 2)),
-        dma((CHUNKS, far_count)), dma((CHUNKS, far_count)), dma((CHUNKS, 2)), dma((CHUNKS, 2)),
+        dma((20,)), dma((grid_rows // (2 * rows),)), dma(pieces), dma(pieces), dma((CHUNKS, 2)), dma((CHUNKS, 2)),
+        dma(pieces), dma(pieces), dma((CHUNKS, 2)), dma((CHUNKS, 2)),
         dma((CHUNKS, 2)), dma((CHUNKS, 2)), dma((1 + grid_rows // (2 * rows),)),
     ]
     hbm = pl.BlockSpec(memory_space=pl.ANY)

time: 35.8 us -> 33.7 us (0.941)
  local copies, waits for them, and re-layouts: 4.91 us -> 2.96 us
    unnamed x8 -> x4, local copies, waits for them, and re-layouts: 4.91 us -> 2.96 us
where the time goes in v2:
time: 33.7 us; the launch traced here: 33.5 us
  Pallas kernels  29.9 us (89%)
  local copies, waits for them, and re-layouts  2.96 us (9%)
  between operations  0.66 us (2%)
    pallas_call x1, Pallas kernels, body(): pl.pallas_call(functools.partial(kernel, groups, devs), out_shape=(jax.Sh...  29.9 us
    unnamed x4, local copies, waits for them, and re-layouts  2.96 us

profile of v2, /device:TPU:1, one launch (start us, length us, event | category | flops | bytes accessed | tf_op | source)
XLA Modules:
  0.0 33.5 jit_solution(17144808322397515417)
XLA Ops:
  0.6 29.9 %step.1 = (bf16[1024,512]{1,0:T(8,128)(2,1)}, bf16[128,512]{1,0:T(8,128)(2,1)}) custom-call(bf16[1024,512]{1,0:T(8,128)(2,1)} %grid_h.1, bf16[128,512]{1,0:T(8,128)(2,1)} %mesh_h.1, bf16[512,512]{1,0:T(8,128)(2,1)} %ee_h.1, bf16[512,512]{1,0:T(8,128)(2,1)} %e1_h.1, bf16[512,512]{1,0:T(8,128)(2,1)} %e2_h.1, bf16[512,512]{1,0:T(8,128)(2,1)} %pe_h.1, ...), custom_call_target="tpu_custom_call" | custom-call | tf_op jit(solution)/shard_map/step/pallas_call | solution.py:373
  30.6 0.0 copy-start
  30.6 2.3 %copy.24 = bf16[1024,512]{1,0:T(8,128)(2,1)} copy(bf16[1024,512]{1,0:T(8,128)(2,1)} %get-tuple-element.4) | data formatting | bytes 2097152
  32.9 0.0 copy-done
  32.9 0.7 %copy.25 = bf16[128,512]{1,0:T(8,128)(2,1)} copy(bf16[128,512]{1,0:T(8,128)(2,1)S(1)} %copy-done) | data formatting | bytes 262144
Async XLA Ops:
  30.6 2.3 %copy-start = (bf16[128,512]{1,0:T(8,128)(2,1)S(1)}, bf16[128,512]{1,0:T(8,128)(2,1)}, u32[]{:S(2)}) copy-start(bf16[128,512]{1,0:T(8,128)(2,1)} %get-tuple-element.5) | copy-start | bytes 393220
